TPU v7x, 32 devices: a whole 2x2x4 slice. The times are simulated.
32 devices in a mesh: model: 8 (over z, y), data: 4 (over x, core).
Axes of the slice: x: 2, y: 2, z: 4, core: 2. Of those that a mesh axis runs over, the one named last changes fastest.
Arguments:
- local_grads: bfloat16 [4, 144, 262144], P('data', None, 'model')
- master: float32 [144, 262144], P(None, ('model', 'data'))
- moment_one: float32 [144, 262144], P(None, ('model', 'data'))
- moment_two: float32 [144, 262144], P(None, ('model', 'data'))
Outputs:
- output 1: bfloat16 [144, 262144], P(None, 'model')
- output 2: float32 [144, 262144], P(None, ('model', 'data'))
- output 3: float32 [144, 262144], P(None, ('model', 'data'))
- output 4: float32 [144, 262144], P(None, ('model', 'data'))
All inputs are finite; a program needn't handle non-finite values.
Results may differ from a plain program's by a relative error of at most 0.001.
Values are sent between devices in bfloat16 or wider.
A program may use at most 1 GiB of HBM per device.

v0:
```python
import jax
import jax.numpy as jnp
from jax import lax
from jax.sharding import PartitionSpec as P

STEP = 4
LEARN_RATE = 0.08
BETA_ONE = 0.9
BETA_TWO = 0.999
EPSILON = 1e-6
WEIGHT_DECAY = 0.01
MAX_NORM = 1.0
CORR_ONE = 1.0 - BETA_ONE ** STEP
CORR_TWO = 1.0 - BETA_TWO ** STEP


def tensor_sums(block_values):
    return jnp.stack([block_values[..., 0:3].sum(axis=-1), block_values[..., 3], block_values[..., 4:8].sum(axis=-1), block_values[..., 8:12].sum(axis=-1)], axis=-1)


def spread_tensors(tensor_values):
    lead_shape = tensor_values.shape[:-1]
    pieces = [jnp.broadcast_to(tensor_values[..., tensor_pos:tensor_pos + 1], lead_shape + (block_count,)) for tensor_pos, block_count in enumerate((3, 1, 4, 4))]
    return jnp.concatenate(pieces, axis=-1)


def adam_direction(grad_mean, clip_scale, master, moment_one, moment_two):
    scaled = clip_scale * grad_mean
    new_one = BETA_ONE * moment_one + (1.0 - BETA_ONE) * scaled
    new_two = BETA_TWO * moment_two + (1.0 - BETA_TWO) * scaled * scaled
    direction = (new_one / CORR_ONE) / (jnp.sqrt(new_two / CORR_TWO) + EPSILON) + WEIGHT_DECAY * master
    return new_one, new_two, direction


def block_ratio(norm_sq):
    tensor_norms = jnp.sqrt(tensor_sums(norm_sq.reshape(2, -1, 12)))
    return spread_tensors(tensor_norms[0] / tensor_norms[1]).reshape(-1, 1)


def solution(mesh):
    data_size = mesh.shape['data']
    both_axes = ('model', 'data')
    state_spec = P(None, both_axes)

    def device_step(local_grads, master, moment_one, moment_two):
        grad_slab = local_grads[0]
        received = lax.all_to_all(grad_slab, 'data', 1, 0, tiled=True)
        grad_mean = jnp.sum(received.reshape(data_size, grad_slab.shape[0], -1), axis=0, dtype=jnp.float32) / data_size
        total_sq = lax.psum(jnp.sum(grad_mean * grad_mean), both_axes)
        clip_scale = jnp.minimum(1.0, MAX_NORM / jnp.sqrt(total_sq))
        new_one, new_two, direction = adam_direction(grad_mean, clip_scale, master, moment_one, moment_two)
        norm_sq = lax.psum(jnp.stack([jnp.sum(master * master, axis=1), jnp.sum(direction * direction, axis=1)]), both_axes)
        new_master = master - LEARN_RATE * block_ratio(norm_sq) * direction
        params = lax.all_gather(new_master.astype(jnp.bfloat16), 'data', axis=1, tiled=True)
        return params, new_master, new_one, new_two

    return jax.shard_map(device_step, mesh=mesh, in_specs=(P('data', None, 'model'), state_spec, state_spec, state_spec), out_specs=(P(None, 'model'), state_spec, state_spec, state_spec), check_vma=False)
```

profile of v0, /device:TPU:0, one launch (start us, length us, event | category | flops | bytes accessed | tf_op | source)
XLA Modules:
  0.0 342.0 jit_solution(14435828469489451495)
XLA Ops:
  7.2 0.0 all-gather.2.cloned.1.call-start
  7.2 16.2 %all_to_all.10 = bf16[144,4,8192]{2,1,0:T(4,128)(2,1)} reshape(bf16[1,144,32768]{2,1,0:T(8,128)(2,1)} %param.4) | data formatting | bytes 18874368 | tf_op jit(solution)/shard_map/all_to_all | solution.py:47
  23.4 12.5 %copy.19 = bf16[144,4,8192]{2,0,1:T(8,128)(2,1)} copy(bf16[144,4,8192]{2,1,0:T(4,128)(2,1)} %all_to_all.10) | data formatting | bytes 18874368 | tf_op jit(solution)/shard_map/all_to_all | solution.py:47
  35.9 112.7 %all_to_all.13 = bf16[144,4,8192]{2,0,1:T(8,128)(2,1)} all-to-all(bf16[144,4,8192]{2,0,1:T(8,128)(2,1)} %copy.19), channel_id=1, replica_groups=mesh['model'=8,'data'=4] {'data'}, dimensions={1} | all-to-all | bytes 18874368 | tf_op jit(solution)/shard_map/all_to_all | solution.py:47
  148.5 6.1 %convert_reduce_fusion = f32[144,8192]{1,0:T(8,128)S(1)} fusion(bf16[144,4,8192]{2,0,1:T(8,128)(2,1)} %all_to_all.13), kind=kLoop, calls=%fused_computation | loop fusion | flops 8257536 | bytes 14155776 | tf_op jit(solution)/shard_map/reduce_sum | solution.py:48
  154.6 0.0 copy-start
  154.6 2.2 copy-done
  156.8 1.8 multiply_reduce_fusion.1
  158.6 40.6 %psum.14 = f32[]{:T(128)} all-reduce(f32[]{:T(128)} %multiply_reduce_fusion.1), channel_id=1, replica_groups=mesh['model'=8,'data'=4] {'model','data'}, use_global_device_ids=true, to_apply=%region_3.0 | all-reduce | flops 1 | bytes 8 | tf_op jit(solution)/shard_map/psum | solution.py:49
  199.9 12.0 %multiply_reduce_fusion.2 = (f32[144]{0:T(256)S(1)}, f32[144]{0:T(256)S(1)}, f32[144,8192]{1,0:T(8,128)}, f32[144,8192]{1,0:T(8,128)}) fusion(f32[144,8192]{1,0:T(8,128)} %param.5, f32[144,8192]{1,0:T(8,128)} %copy-done, f32[]{:T(128)S(6)} %mul.76, f32[144,8192]{1,0:T(8,128)} %param.6, f32[144,8192]{1,0:T(8,128)} %param.7), kind=kLoop, calls=%fused_computation.8 | loop fusion | flops 21233376 | bytes 28312708 | tf_op jit(solution)/shard_map/reduce_sum | solution.py:52
  211.9 0.1 reshape.28
  212.0 41.3 %psum.15 = f32[2,12,12]{2,1,0:T(8,128)S(1)} all-reduce(f32[2,12,12]{2,1,0:T(8,128)S(1)} %reshape.28), channel_id=1, replica_groups=mesh['model'=8,'data'=4] {'model','data'}, use_global_device_ids=true, to_apply=%region_5.0 | all-reduce | flops 288 | bytes 2304 | tf_op jit(solution)/shard_map/psum | solution.py:52
  253.3 0.1 slice_reduce_fusion.2
  253.4 0.2 slice_reduce_fusion.1
  253.6 0.1 slice.41
  253.6 0.1 copy.21
  253.8 0.1 copy.24
  253.9 0.1 broadcast_in_dim.22
  254.0 0.1 broadcast_in_dim.26
  254.0 0.1 broadcast_in_dim.24
  254.1 0.1 maximum_multiply_fusion
  254.2 0.1 mul.91
  254.3 8.2 %fusion.2 = (bf16[144,8192]{1,0:T(8,128)(2,1)}, f32[144,8192]{1,0:T(8,128)}) fusion(f32[144,8192]{1,0:T(8,128)} %param.5, f32[144,8192]{1,0:T(8,128)} %get-tuple-element.23, f32[144,8192]{1,0:T(8,128)} %get-tuple-element.22, f32[144]{0:T(256)S(1)} %mul.91), kind=kLoop, calls=%fused_computation.20 | loop fusion | flops 10616832 | bytes 21234240 | tf_op jit(solution)/shard_map/convert_element_type | solution.py:54
  262.5 0.0 all-gather.2.cloned.1.call-update
  262.5 64.5 %all-gather.2.cloned.1.call-done = bf16[144,32768]{1,0:T(8,128)(2,1)} async-done(((bf16[144,8192]{1,0:T(8,128)(2,1)}), bf16[144,32768]{1,0:T(8,128)(2,1)}) %all-gather.2.cloned.1.call-update) | async-done | bytes 9437200 | tf_op jit(solution)/shard_map/all_gather | solution.py:54
  327.0 8.2 %copy.26 = bf16[144,32768]{1,0:T(8,128)(2,1)} copy(bf16[144,32768]{1,0:T(8,128)(2,1)} %all-gather.2.cloned.1.call-done) | data formatting | bytes 18874368
  (4 shorter events, 0.0 us)
Async XLA Ops:
  7.2 319.8 %all-gather.2.cloned.1.call-start = ((), (), s32[]{:S(2)}) async-start(), calls=%async_computation.1 | async-start | bytes 11796480 | tf_op jit(solution)/shard_map/all_gather | solution.py:54
  154.6 2.2 copy-start
Sparse Core Ops, SparseCore 0:
  262.6 64.2 all-gather.1
where the time goes:
time: 343 us; the launch traced here: 342 us
  blocking collectives  195 us (57%)
  waiting for transfers between devices  64.5 us (19%)
  local copies, waits for them, and re-layouts  39.7 us (12%)
  other arithmetic  28.4 us (8%)
  between operations  14.8 us (4%)
    all_to_all x1, blocking collectives, device_step(): received = lax.all_to_all(grad_slab, 'data', 1, 0, tiled=True)  113 us
    all_gather x1, waiting for transfers between devices, device_step(): lax.all_gather(new_master.astype(jnp.bfloat16), 'data', axis=1, tiled=True)  64.5 us
    psum x1, blocking collectives, device_step(): lax.psum(jnp.stack([jnp.sum(master * master, axis=1), jnp.sum(direction *...  41.3 us
    psum x1, blocking collectives, device_step(): total_sq = lax.psum(jnp.sum(grad_mean * grad_mean), both_axes)  40.6 us
    all_to_all x2, local copies, waits for them, and re-layouts, device_step(): received = lax.all_to_all(grad_slab, 'data', 1, 0, tiled=True)  28.6 us
    reduce_sum x1, other arithmetic, device_step(): jnp.sum(master * master, axis=1)  12 us
    unnamed x3, local copies, waits for them, and re-layouts  10.4 us
    convert_element_type x1, other arithmetic, device_step(): new_master.astype(jnp.bfloat16)  8.19 us
  transfers between devices with their start and end apart: 1, of which 1 were waited for; matrix products, arithmetic and copies ran while one was open for 0% of the time, Pallas kernels for 0%

commit v1 on v0

v1 whole, which is shorter than its diff:
```python
import functools

import jax
import jax.numpy as jnp
from jax import lax
from jax.experimental import pallas as pl
from jax.experimental.pallas import tpu as pltpu
from jax.sharding import PartitionSpec as P

STEP = 4
LEARN_RATE = 0.08
BETA_ONE = 0.9
BETA_TWO = 0.999
EPSILON = 1e-6
WEIGHT_DECAY = 0.01
MAX_NORM = 1.0
CORR_ONE = 1.0 - BETA_ONE ** STEP
CORR_TWO = 1.0 - BETA_TWO ** STEP

MESH = pl.DeviceIdType.MESH
LANES = 128
SUBLANES = 8
CHUNK_ROWS = 16
SUM_COLS = 512
STEP_COLS = 1024
BLOCKS_PER_LAYER = 12
TENSOR_STARTS = (0, 3, 4, 8)


def lane_fold(values):
    total = values[:, :LANES]
    for start in range(LANES, values.shape[1], LANES):
        total = total + values[:, start:start + LANES]
    return total


def tensor_mask(rows):
    row = lax.broadcasted_iota(jnp.int32, (rows, LANES), 0)
    lane = lax.broadcasted_iota(jnp.int32, (rows, LANES), 1)
    layer = row // BLOCKS_PER_LAYER
    block = row - layer * BLOCKS_PER_LAYER
    tensor = layer * len(TENSOR_STARTS)
    for start in TENSOR_STARTS[1:]:
        tensor = tensor + (block >= start).astype(jnp.int32)
    return tensor == lane


def step_kernel(model_size, data_size, grads, master, moment_one, moment_two,
                new_params, new_master, new_one, new_two,
                gathered, grad_mean, row_sq, row_scale, clip_rows, norm_rows,
                load_sem, own_sem, sum_send, sum_recv, small_send, small_recv,
                out_send, out_recv, fwd_send, fwd_recv):
    rows, width = new_master.shape
    chunks = rows // CHUNK_ROWS
    devices = model_size * data_size
    my_model = lax.axis_index('model')
    my_data = lax.axis_index('data')
    me = my_model * data_size + my_data
    partner = my_data + 1 - 2 * lax.rem(my_data, 2)
    across = lax.rem(my_data + 2, data_size)
    across_partner = lax.rem(partner + 2, data_size)
    peers = (my_data, partner, across, across_partner)

    def device_at(index):
        return (index // data_size, lax.rem(index, data_size))

    loads = [pltpu.make_async_copy(src, dst, load_sem.at[i]) for i, (src, dst) in enumerate(
        ((master, new_master), (moment_one, new_one), (moment_two, new_two)))]

    barrier = pltpu.get_barrier_semaphore()

    @pl.loop(1, devices)
    def _(offset):
        pl.semaphore_signal(barrier, inc=1, device_id=device_at(lax.rem(me + offset, devices)), device_id_type=MESH)
    pl.semaphore_wait(barrier, devices - 1)

    def grad_part(slot, chunk):
        return grads.at[0, pl.ds(chunk * CHUNK_ROWS, CHUNK_ROWS), pl.ds(pl.multiple_of(peers[slot] * width, LANES), width)]

    def slot_part(slot, chunk):
        return gathered.at[slot, pl.ds(chunk * CHUNK_ROWS, CHUNK_ROWS)]

    def own_copy(chunk):
        return pltpu.make_async_copy(grad_part(0, chunk), slot_part(0, chunk), own_sem.at[chunk])

    def grad_copy(slot, chunk):
        return pltpu.make_async_remote_copy(grad_part(slot, chunk), slot_part(slot, chunk), sum_send.at[slot], sum_recv.at[slot, chunk], device_id=(my_model, peers[slot]), device_id_type=MESH)

    @pl.loop(0, chunks)
    def _(chunk):
        for slot in (2, 3, 1):
            grad_copy(slot, chunk).start()
        own_copy(chunk).start()

    for load in loads:
        load.start()
    for load in loads:
        load.wait()

    mask = tensor_mask(rows)

    def square_rows(ref):
        @pl.loop(0, rows // SUBLANES)
        def _(group):
            row = pl.ds(pl.multiple_of(group * SUBLANES, SUBLANES), SUBLANES)

            def fold(block, total):
                part = ref[row, pl.ds(pl.multiple_of(block * STEP_COLS, LANES), STEP_COLS)]
                return total + lane_fold(part * part)
            row_sq[row, :] = lax.fori_loop(0, width // STEP_COLS, fold, jnp.zeros((SUBLANES, LANES), jnp.float32))

    def tensor_row():
        per_row = jnp.sum(row_sq[...], axis=1, keepdims=True)
        return jnp.sum(jnp.where(mask, per_row, 0.0), axis=0, keepdims=True)

    def small_copy(which, table, target):
        return pltpu.make_async_remote_copy(table.at[pl.ds(me, 1)], table.at[pl.ds(me, 1)], small_send.at[which], small_recv.at[which], device_id=device_at(target), device_id_type=MESH)

    def send_row(which, table, row):
        table[pl.ds(me, 1), :] = row

        @pl.loop(1, devices)
        def _(offset):
            small_copy(which, table, lax.rem(me + offset, devices)).start()

    def all_rows(which, table):
        rest = table.at[pl.ds(0, devices - 1)]
        pltpu.make_async_remote_copy(rest, rest, small_send.at[which], small_recv.at[which], device_id=(my_model, my_data), device_id_type=MESH).wait()
        return jnp.sum(table[...], axis=0, keepdims=True)

    square_rows(new_master)
    send_row(0, norm_rows.at[0], tensor_row())

    def add_chunk(chunk, total):
        own_copy(chunk).wait()
        for slot in (1, 2, 3):
            grad_copy(slot, chunk).wait_recv()
        row = pl.ds(pl.multiple_of(chunk * CHUNK_ROWS, CHUNK_ROWS), CHUNK_ROWS)

        def add_block(block, total):
            col = pl.ds(pl.multiple_of(block * SUM_COLS, LANES), SUM_COLS)
            part = [gathered[slot, row, col].astype(jnp.float32) for slot in range(data_size)]
            mean = ((part[0] + part[1]) + (part[2] + part[3])) * (1.0 / data_size)
            grad_mean[row, col] = mean
            return total + lane_fold(mean * mean)
        return lax.fori_loop(0, width // SUM_COLS, add_block, total)

    grad_sq = lax.fori_loop(0, chunks, add_chunk, jnp.zeros((CHUNK_ROWS, LANES), jnp.float32))
    send_row(1, clip_rows, jnp.sum(grad_sq, axis=0, keepdims=True))
    total_sq = jnp.sum(all_rows(1, clip_rows), axis=1, keepdims=True)
    clip = jnp.minimum(1.0, MAX_NORM / jnp.sqrt(total_sq))
    one_scale = jnp.broadcast_to((1.0 - BETA_ONE) * clip, (SUBLANES, STEP_COLS))
    two_scale = jnp.broadcast_to((1.0 - BETA_TWO) * clip * clip, (SUBLANES, STEP_COLS))

    @pl.loop(0, rows // SUBLANES)
    def _(group):
        row = pl.ds(pl.multiple_of(group * SUBLANES, SUBLANES), SUBLANES)

        def step_block(block, total):
            col = pl.ds(pl.multiple_of(block * STEP_COLS, LANES), STEP_COLS)
            grad = grad_mean[row, col]
            one = BETA_ONE * new_one[row, col] + one_scale * grad
            two = BETA_TWO * new_two[row, col] + two_scale * grad * grad
            new_one[row, col] = one
            new_two[row, col] = two
            direction = (one * (1.0 / CORR_ONE)) / (jnp.sqrt(two * (1.0 / CORR_TWO)) + EPSILON) + WEIGHT_DECAY * new_master[row, col]
            grad_mean[row, col] = direction
            return total + lane_fold(direction * direction)
        row_sq[row, :] = lax.fori_loop(0, width // STEP_COLS, step_block, jnp.zeros((SUBLANES, LANES), jnp.float32))

    send_row(2, norm_rows.at[1], tensor_row())
    weight_sq = all_rows(0, norm_rows.at[0])
    step_sq = all_rows(2, norm_rows.at[1])
    ratio = LEARN_RATE * (jnp.sqrt(weight_sq) / jnp.sqrt(step_sq))
    scale = jnp.sum(jnp.where(mask, ratio, 0.0), axis=1, keepdims=True)
    row_scale[...] = jnp.broadcast_to(scale, (rows, LANES))

    my_col = pl.multiple_of(my_data * width, LANES)

    def update_chunk(chunk):
        row = pl.ds(pl.multiple_of(chunk * CHUNK_ROWS, CHUNK_ROWS), CHUNK_ROWS)
        rate = jnp.broadcast_to(row_scale[row, 0:1], (CHUNK_ROWS, SUM_COLS))

        @pl.loop(0, width // SUM_COLS)
        def _(block):
            start = pl.multiple_of(block * SUM_COLS, LANES)
            col = pl.ds(start, SUM_COLS)
            updated = new_master[row, col] - rate * grad_mean[row, col]
            new_master[row, col] = updated
            new_params[row, pl.ds(pl.multiple_of(my_col + start, LANES), SUM_COLS)] = updated.astype(jnp.bfloat16)

    def params_part(owner, chunk):
        return new_params.at[pl.ds(chunk * CHUNK_ROWS, CHUNK_ROWS), pl.ds(pl.multiple_of(owner * width, LANES), width)]

    def params_copy(owner, target, chunk, send, recv):
        part = params_part(owner, chunk)
        return pltpu.make_async_remote_copy(part, part, send, recv, device_id=(my_model, target), device_id_type=MESH)

    def across_copy(chunk):
        return params_copy(my_data, across, chunk, out_send.at[0], out_recv.at[0, chunk])

    def partner_copy(chunk):
        return params_copy(my_data, partner, chunk, out_send.at[1], out_recv.at[1, chunk])

    def forward_copy(chunk):
        return params_copy(across, partner, chunk, fwd_send.at[0], fwd_recv.at[chunk])

    update_chunk(0)

    @pl.loop(1, chunks)
    def _(chunk):
        update_chunk(chunk)
        across_copy(chunk - 1).start()
        partner_copy(chunk - 1).start()
    across_copy(chunks - 1).start()
    partner_copy(chunks - 1).start()

    @pl.loop(0, chunks)
    def _(chunk):
        across_copy(chunk).wait_recv()
        forward_copy(chunk).start()

    @pl.loop(0, chunks)
    def _(chunk):
        partner_copy(chunk).wait_recv()
        forward_copy(chunk).wait_recv()

    whole = new_params.at[:, pl.ds(0, width)]
    for send in (out_send.at[0], out_send.at[1], fwd_send.at[0]):
        pltpu.make_async_remote_copy(whole, whole, send, out_recv.at[0, 0], device_id=(my_model, partner), device_id_type=MESH).wait_send()
    for slot in (1, 2, 3):
        pltpu.make_async_remote_copy(gathered.at[0], gathered.at[0], sum_send.at[slot], out_recv.at[0, 0], device_id=(my_model, partner), device_id_type=MESH).wait_send()


def write_kernel(count, *refs):
    sources, targets, sems = refs[:count], refs[count:2 * count], refs[2 * count]
    copies = [pltpu.make_async_copy(src, dst, sems.at[i]) for i, (src, dst) in enumerate(zip(sources, targets))]
    for copy in copies:
        copy.start()
    for copy in copies:
        copy.wait()


def solution(mesh):
    model_size, data_size = mesh.shape['model'], mesh.shape['data']
    devices = model_size * data_size
    state_spec = P(None, ('model', 'data'))

    def device_step(local_grads, master, moment_one, moment_two):
        rows, width = master.shape
        chunks = rows // CHUNK_ROWS
        hbm = pl.BlockSpec(memory_space=pltpu.HBM)
        vmem = pl.BlockSpec(memory_space=pltpu.VMEM)
        state = pltpu.VMEM((rows, width), jnp.float32)
        held = pl.pallas_call(
            functools.partial(step_kernel, model_size, data_size),
            out_shape=(pltpu.VMEM((rows, width * data_size), jnp.bfloat16), state, state, state),
            in_specs=[hbm] * 4,
            out_specs=[vmem] * 4,
            scratch_shapes=[
                pltpu.VMEM((data_size, rows, width), jnp.bfloat16),
                pltpu.VMEM((rows, width), jnp.float32),
                pltpu.VMEM((rows, LANES), jnp.float32),
                pltpu.VMEM((rows, LANES), jnp.float32),
                pltpu.VMEM((devices, LANES), jnp.float32),
                pltpu.VMEM((2, devices, LANES), jnp.float32),
                pltpu.SemaphoreType.DMA((3,)),
                pltpu.SemaphoreType.DMA((chunks,)),
                pltpu.SemaphoreType.DMA((data_size,)),
                pltpu.SemaphoreType.DMA((data_size, chunks)),
                pltpu.SemaphoreType.DMA((3,)),
                pltpu.SemaphoreType.DMA((3,)),
                pltpu.SemaphoreType.DMA((2,)),
                pltpu.SemaphoreType.DMA((2, chunks)),
                pltpu.SemaphoreType.DMA((1,)),
                pltpu.SemaphoreType.DMA((chunks,)),
            ],
            compiler_params=pltpu.CompilerParams(collective_id=0, has_side_effects=True, vmem_limit_bytes=38 * 2 ** 20),
            name='lamb_step',
        )(local_grads, master, moment_one, moment_two)
        return pl.pallas_call(
            functools.partial(write_kernel, len(held)),
            out_shape=tuple(jax.ShapeDtypeStruct(a.shape, a.dtype) for a in held),
            in_specs=[vmem] * len(held),
            out_specs=[hbm] * len(held),
            scratch_shapes=[pltpu.SemaphoreType.DMA((len(held),))],
            compiler_params=pltpu.CompilerParams(vmem_limit_bytes=2 ** 20),
            name='write_out',
        )(*held)

    return jax.shard_map(device_step, mesh=mesh, in_specs=(P('data', None, 'model'), state_spec, state_spec, state_spec), out_specs=(P(None, 'model'), state_spec, state_spec, state_spec), check_vma=False)
```

time: 343 us -> 190 us (0.55)
  blocking collectives: 195 us -> 0 us
  Pallas kernels: 0 us -> 189 us
  waiting for transfers between devices: 64.5 us -> 0 us
  local copies, waits for them, and re-layouts: 39.7 us -> 0 us
  other arithmetic: 28.4 us -> 0 us
  between operations: 14.8 us -> 0.64 us
    pallas_call x0 -> x2, Pallas kernels: none -> 189 us  [the longest x1 181 us: device_step(): pl.pallas_call(functools.partial(step_kernel, model_size, data_size), out...]
    all_to_all x1 -> x0, blocking collectives: 113 us -> none  [device_step(): received = lax.all_to_all(grad_slab, 'data', 1, 0, tiled=True)]
    psum x2 -> x0, blocking collectives: 81.9 us -> none  [the longest x1 41.3 us: device_step(): lax.psum(jnp.stack([jnp.sum(master * master, axis=1), jnp.sum(direction *...]
    all_gather x1 -> x0, waiting for transfers between devices: 64.5 us -> none  [device_step(): lax.all_gather(new_master.astype(jnp.bfloat16), 'data', axis=1, tiled=True)]
    all_to_all x2 -> x0, local copies, waits for them, and re-layouts: 28.6 us -> none  [device_step(): received = lax.all_to_all(grad_slab, 'data', 1, 0, tiled=True)]
    reduce_sum x5 -> x0, other arithmetic: 20.1 us -> none  [the longest x1 12 us: device_step(): jnp.sum(master * master, axis=1)]
    unnamed x3 -> x0, local copies, waits for them, and re-layouts: 10.4 us -> none
    convert_element_type x1 -> x0, other arithmetic: 8.19 us -> none  [device_step(): new_master.astype(jnp.bfloat16)]
  transfers between devices with their start and end apart: 1 -> 0, of which waited for: 1 -> 0; matrix products, arithmetic and copies ran while one was open for 0% -> 0% of each run, Pallas kernels for 0% -> 0%
where the time goes in v1:
time: 190 us; the launch traced here: 189 us
  Pallas kernels  189 us (99%)
    pallas_call x1, Pallas kernels, device_step(): pl.pallas_call(functools.partial(step_kernel, model_size, data_size), out...  181 us
    pallas_call x1, Pallas kernels, device_step(): pl.pallas_call(functools.partial(write_kernel, len(held)), out_shape=tupl...  8.17 us

profile of v1, /device:TPU:0, one launch (start us, length us, event | category | flops | bytes accessed | tf_op | source)
XLA Modules:
  0.0 189.4 jit_solution(17607819105010185483)
XLA Ops:
  0.6 180.6 %lamb_step.1 = (bf16[144,32768]{1,0:T(8,128)(2,1)S(1)}, f32[144,8192]{1,0:T(8,128)S(1)}, f32[144,8192]{1,0:T(8,128)S(1)}, f32[144,8192]{1,0:T(8,128)S(1)}) custom-call(bf16[1,144,32768]{2,1,0:T(8,128)(2,1)} %grads.1, f32[144,8192]{1,0:T(8,128)} %master.1, f32[144,8192]{1,0:T(8,128)} %moment_one.1, f32[144,8192]{1,0:T(8,128)} %moment_two.1), custom_call_target="tpu_custom_call" | custom-call | tf_op jit(solution)/shard_map/lamb_step/pallas_call | solution.py:255
  181.2 8.2 %write_out.1 = (bf16[144,32768]{1,0:T(8,128)(2,1)}, f32[144,8192]{1,0:T(8,128)}, f32[144,8192]{1,0:T(8,128)}, f32[144,8192]{1,0:T(8,128)}) custom-call(bf16[144,32768]{1,0:T(8,128)(2,1)S(1)} %get-tuple-element.8.refs_0_, f32[144,8192]{1,0:T(8,128)S(1)} %get-tuple-element.9.refs_1_, f32[144,8192]{1,0:T(8,128)S(1)} %get-tuple-element.10.refs_2_, ...), custom_call_target="tpu_custom_call" | custom-call | tf_op jit(solution)/shard_map/write_out/pallas_call | solution.py:281
